TPU v7x, 32 devices: a whole 2x2x4 slice. The times are simulated.
32 devices in a mesh: lat: 8 (over z, y), ch: 4 (over x, core).
Axes of the slice: x: 2, y: 2, z: 4, core: 2. Of those that a mesh axis runs over, the one named last changes fastest.
Arguments:
- field: bfloat16 [728, 256, 1440], P('lat', 'ch'), may hold values from -6 to 6
- legendre: bfloat16 [384, 721, 728], P(('lat', 'ch')), may hold values from -0.21875 to 0.21875
- pair_order: int32 [384], replicated, may hold values from 0 to 383, each once
Outputs:
- coeffs: float32 [384, 721, 2, 256], P(('lat', 'ch'))
Inputs may be any that keep to these rules, and one draw needn't show every extreme that they name: `pair_order`: each of 0 to 383 appears once; a value p below 360 gives its bin the orders p and 719 - p, and a bin with a larger value is empty.
All inputs are finite; a program needn't handle non-finite values.
Results may differ from a plain program's by a relative error of at most 0.0037.
Values may be sent and summed in bfloat16 or wider, within the bound.
A program may use at most 256 MiB of HBM per device.

v0:
```python
import math
import jax
import jax.numpy as jnp
from jax import lax
from jax.sharding import PartitionSpec as P

NLAT = 721


def dft_table(points, modes, lon_count):
    turns = points[:, None] * modes[None, :] % lon_count
    angle = turns.astype(jnp.float32) * (2.0 * math.pi / lon_count)
    return jnp.stack([jnp.cos(angle), -jnp.sin(angle)], axis=-1).astype(jnp.bfloat16)


def project(basis_piece, data_rows, boundary, keep_mask):
    products = jnp.einsum(
        "brl,lbn->brn", basis_piece, data_rows, preferred_element_type=jnp.float32
    )
    bin_count, row_count, width_all = products.shape
    products = products.reshape(bin_count, row_count, 2, 2, width_all // 4)
    degree = jnp.arange(row_count, dtype=jnp.int32)
    upper_part = degree[None, :, None, None] < boundary[:, None, None, None]
    chosen = jnp.where(upper_part, products[:, :, 0], products[:, :, 1])
    return chosen * keep_mask[:, None, None, None].astype(jnp.float32)


def per_device(field, legendre, pair_order):
    lat_rows, chan_dev, lon_count = field.shape
    slot_count = pair_order.shape[0]
    lat_count = lax.axis_size("lat")
    group_size = slot_count // lat_count
    max_order = legendre.shape[1] - 1
    keep_all = pair_order < max_order // 2
    first_order = jnp.where(keep_all, pair_order, 0)
    orders = jnp.stack([first_order, max_order - 1 - first_order], axis=1)
    bound_all = max_order - first_order
    rows_global = lax.axis_index("lat") * lat_rows + jnp.arange(lat_rows, dtype=jnp.int32)
    masked = jnp.where((rows_global < NLAT)[:, None, None], field, jnp.zeros_like(field))
    norm_scale = 2.0 * math.pi / lon_count
    points = jnp.arange(lon_count, dtype=jnp.int32)
    dft_basis = dft_table(points, orders.reshape(-1), lon_count).reshape(lon_count, 4 * slot_count)
    fourier = jnp.einsum("ack,kn->anc", masked, dft_basis, preferred_element_type=jnp.float32)
    fourier = (fourier * norm_scale).astype(jnp.bfloat16).reshape(lat_rows, slot_count, 4, chan_dev)
    received = lax.all_to_all(
        fourier.reshape(lat_rows, slot_count, 4 * chan_dev),
        "lat",
        split_axis=1,
        concat_axis=0,
        tiled=True,
    )
    group_start = lax.axis_index("lat") * group_size
    bound_group = lax.dynamic_slice_in_dim(bound_all, group_start, group_size)
    keep_group = lax.dynamic_slice_in_dim(keep_all, group_start, group_size)
    part_sums = project(
        lax.all_gather(legendre, "ch", axis=0, tiled=True), received, bound_group, keep_group
    )
    return lax.all_to_all(part_sums, "ch", split_axis=0, concat_axis=3, tiled=True)


def solution(mesh):
    in_specs = (P("lat", "ch", None), P(("lat", "ch"), None, None), P())
    out_specs = P(("lat", "ch"), None, None, None)
    return jax.shard_map(
        per_device, mesh=mesh, in_specs=in_specs, out_specs=out_specs, check_vma=False
    )
```

profile of v0, /device:TPU:0, one launch (start us, length us, event | category | flops | bytes accessed | tf_op | source)
XLA Modules:
  0.0 950.9 jit_solution(16822089257262218695)
XLA Ops:
  6.5 0.0 all-gather.2.cloned.1.call-start
  6.5 0.7 all-gather.2.cloned.1.call-update
  7.3 0.7 broadcast_subtract_fusion.1
  8.0 0.1 copy.30
  8.1 0.1 mul.66
  8.3 19.0 %cosine_convert_fusion = (bf16[1440,768,1]{1,0,2:T(8,128)(2,1)S(1)}, bf16[1440,768,1]{1,0,2:T(8,128)(2,1)S(1)}) fusion(s32[768]{0:T(1024)S(1)} %mul.66), kind=kLoop, calls=%fused_computation.18 | loop fusion | flops 13271040 | bytes 4426752 | tf_op jit(solution)/shard_map/convert
  27.3 3.2 pad_maximum_fusion
  30.6 13.2 %copy.31 = bf16[1440,768,2]{0,2,1:T(2,128)(2,1)} copy(bf16[1440,768,2]{1,0,2:T(8,128)(2,1)} %pad_maximum_fusion) | data formatting | bytes 8847360 | tf_op jit(solution)/shard_map/stack | solution.py:13
  43.8 10.9 %convert_element_type.30 = bf16[1440,1536]{0,1:T(8,128)(2,1)} reshape(bf16[1440,768,2]{0,2,1:T(2,128)(2,1)} %copy.31) | data formatting | bytes 8847360 | tf_op jit(solution)/shard_map/convert_element_type | solution.py:13
  54.7 0.0 copy-start
  54.7 16.6 %broadcast_select_fusion = bf16[91,64,1440]{2,1,0:T(8,128)(2,1)} fusion(bf16[91,64,1440]{2,1,0:T(8,128)(2,1)} %param.3, pred[91]{0:T(512)(128)(4,1)S(1)} %add_compare_fusion), kind=kLoop, calls=%fused_computation.10 | loop fusion | flops 8386560 | bytes 33546332 | tf_op jit(solution)/shard_map/jit(_where)/select_n | solution.py:39
  71.3 0.0 copy-done
  71.3 49.8 %fusion = bf16[91,1536,64]{1,0,2:T(8,128)(2,1)} fusion(bf16[91,64,1440]{2,1,0:T(8,128)(2,1)} %broadcast_select_fusion, bf16[1440,1536]{0,1:T(8,128)(2,1)S(1)} %copy-done), kind=kOutput, calls=%fused_computation.1 | convolution fusion | flops 25781403648 | bytes 39088128 | tf_op jit(solution)/shard_map/ack,kn->anc/dot_general | solution.py:43
  121.2 31.3 %copy.34 = bf16[91,1536,64]{0,2,1:T(8,128)(2,1)} copy(bf16[91,1536,64]{1,0,2:T(8,128)(2,1)} %fusion) | data formatting | bytes 35782656 | tf_op jit(solution)/shard_map/convert_element_type | solution.py:44
  152.5 28.4 %copy.35 = bf16[91,384,256]{2,0,1:T(8,128)(2,1)} copy(bf16[91,384,256]{0,2,1:T(8,128)(2,1)} %bitcast.33) | data formatting | bytes 35782656 | tf_op jit(solution)/shard_map/reshape;reshape | solution.py:46
  180.9 0.0 copy-start.1
  180.9 7.3 all-to-all-start
  188.1 0.1 dynamic_slice.6
  188.2 0.0 copy-done.1
  188.2 0.1 dynamic-slice_convert_fusion
  188.3 0.1 iota_compare_fusion
  188.4 408.6 %all-to-all-done = bf16[91,384,256]{2,0,1:T(8,128)(2,1)} async-done(((bf16[91,384,256]{2,0,1:T(8,128)(2,1)}), bf16[91,384,256]{2,0,1:T(8,128)(2,1)}, u32[]{:S(2)}, u32[]{:S(2)}) %all-to-all-start) | async-done | bytes 17891360 | tf_op jit(solution)/shard_map/all_to_all | solution.py:45
  596.9 19.0 %copy.37 = bf16[8,91,48,256]{3,2,1,0:T(8,128)(2,1)} copy(bf16[8,91,48,256]{3,1,2,0:T(8,128)(2,1)} %bitcast.5) | data formatting | bytes 35782656 | tf_op jit(solution)/shard_map/all_to_all | solution.py:45
  615.9 0.0 all-gather.2.cloned.1.call-done
  615.9 36.0 %fusion.9 = f32[48,721,256]{2,1,0:T(8,128)} fusion(bf16[48,721,728]{2,1,0:T(8,128)(2,1)} %all-gather.2.cloned.1.call-done, bf16[728,48,256]{2,1,0:T(8,128)(2,1)} %bitcast.36), kind=kOutput, calls=%fused_computation.11 | convolution fusion | flops 12899647488 | bytes 103719168 | tf_op jit(solution)/shard_map/brl,lbn->brn/dot_general | solution.py:17
  651.9 36.0 %copy.39 = f32[48,721,256]{1,2,0:T(8,128)} copy(f32[48,721,256]{2,1,0:T(8,128)} %fusion.9) | data formatting | bytes 70877184 | tf_op jit(solution)/shard_map/brl,lbn->brn/dot_general | solution.py:17
  687.9 12.8 %fusion.2 = f32[48,721,2,64]{1,3,2,0:T(8,128)S(1)} fusion(f32[48,721,2,2,64]{1,4,3,2,0:T(8,128)} %bitcast.32, f32[48]{0:T(128)S(1)} %dynamic-slice_convert_fusion, pred[48,721]{1,0:T(8,128)(4,1)S(1)} %iota_compare_fusion), kind=kLoop, calls=%fused_computation.4 | loop fusion | flops 8859648 | bytes 53192688 | tf_op jit(solution)/shard_map/mul | solution.py:25
  700.8 208.6 %all_to_all.36 = f32[48,721,2,64]{1,3,2,0:T(8,128)S(1)} all-to-all(f32[48,721,2,64]{1,3,2,0:T(8,128)S(1)} %fusion.2), channel_id=1, replica_groups=mesh['lat'=8,'ch'=4] {'ch'}, dimensions={0} | all-to-all | bytes 35438592 | tf_op jit(solution)/shard_map/all_to_all | solution.py:58
  909.4 6.9 copy.41
  916.4 27.7 %copy.42 = f32[12,721,2,256]{3,2,1,0:T(2,128)} copy(f32[12,721,2,256]{1,3,2,0:T(8,128)} %bitcast.35) | data formatting | bytes 35438592 | tf_op jit(solution)/shard_map/all_to_all | solution.py:58
  (5 shorter events, 0.0 us)
Async XLA Ops:
  6.5 609.4 %all-gather.2.cloned.1.call-start = ((), (), s32[]{:S(2)}) async-start(), calls=%async_computation.2 | async-start | bytes 67092480 | tf_op jit(solution)/shard_map/all_gather | solution.py:56
  54.7 16.6 %copy-start = (bf16[1440,1536]{0,1:T(8,128)(2,1)S(1)}, bf16[1440,1536]{0,1:T(8,128)(2,1)}, u32[]{:S(2)}) copy-start(bf16[1440,1536]{0,1:T(8,128)(2,1)} %convert_element_type.30) | copy-start | bytes 13271044
  180.9 7.3 copy-start.1
  180.9 416.1 %all-to-all-start = ((bf16[91,384,256]{2,0,1:T(8,128)(2,1)}), bf16[91,384,256]{2,0,1:T(8,128)(2,1)}, u32[]{:S(2)}, u32[]{:S(2)}) async-start(bf16[91,384,256]{2,0,1:T(8,128)(2,1)} %copy.35), calls=%async_computation | async-start | bytes 37748736 | tf_op jit(solution)/shard_map/all_to_all | solution.py:45
Sparse Core Ops, SparseCore 0:
  8.9 320.7 all-gather.1
where the time goes:
time: 955 us; the launch traced here: 951 us
  waiting for transfers between devices  409 us (43%)
  blocking collectives  209 us (22%)
  local copies, waits for them, and re-layouts  174 us (18%)
  matrix products  85.8 us (9%)
  other arithmetic  52.6 us (6%)
  between operations  13.4 us (1%)
    all_to_all x1, waiting for transfers between devices, per_device(): lax.all_to_all(fourier.reshape(lat_rows, slot_count, 4 * chan_dev), 'lat'...  409 us
    all_to_all x1, blocking collectives, per_device(): lax.all_to_all(part_sums, 'ch', split_axis=0, concat_axis=3, tiled=True)  209 us
    dot_general x1, matrix products, per_device(): jnp.einsum('ack,kn->anc', masked, dft_basis, preferred_element_type=jnp.f...  49.8 us
    dot_general x1, local copies, waits for them, and re-layouts, project(): jnp.einsum('brl,lbn->brn', basis_piece, data_rows, preferred_element_type...  36 us
    dot_general x1, matrix products, project(): jnp.einsum('brl,lbn->brn', basis_piece, data_rows, preferred_element_type...  36 us
    all_to_all x2, local copies, waits for them, and re-layouts, per_device(): lax.all_to_all(part_sums, 'ch', split_axis=0, concat_axis=3, tiled=True)  34.7 us
    convert_element_type x1, local copies, waits for them, and re-layouts, per_device(): (fourier * norm_scale).astype(jnp.bfloat16)  31.3 us
    another operation x1, local copies, waits for them, and re-layouts, per_device(): fourier.reshape(lat_rows, slot_count, 4 * chan_dev)  28.4 us
  transfers between devices with their start and end apart: 2, of which 1 were waited for; matrix products, arithmetic and copies ran while one was open for 20% of the time, Pallas kernels for 0%

commit v1 on v0

--- a/solution.py
+++ b/solution.py
@@ -1,3 +1,4 @@
+import functools
 import math
 import jax
 import jax.numpy as jnp
@@ -5,6 +6,37 @@
 from jax.sharding import PartitionSpec as P
 
 NLAT = 721
+
+
+def view_patch_now(here_x, dim_k, own_rows):
+    b_next = here_x.shape
+    reached = here_x.reshape(
+        *b_next[:dim_k], own_rows, b_next[dim_k] // own_rows, *b_next[dim_k + 1 :]
+    )
+    return jnp.moveaxis(reached, dim_k, 0)
+
+
+def rings_replace(point, row_dim):
+    point = jnp.moveaxis(point, 0, row_dim)
+    opened = point.shape
+    return point.reshape(
+        *opened[:row_dim], opened[row_dim] * opened[row_dim + 1], *opened[row_dim + 2 :]
+    )
+
+
+def search_the_views(target, which_axis, block_here, local_array):
+    val2, row_out = (lax.axis_size(which_axis), lax.axis_index(which_axis))
+    small = view_patch_now(target, block_here, val2)
+    d_next = small
+    for dev in range(1, val2):
+        prior, block_now = ((row_out + dev) % val2, (row_out - dev) % val2)
+        y = lax.dynamic_index_in_dim(small, prior, 0)
+        all_rows = lax.ppermute(y, which_axis, [(j, (j + dev) % val2) for j in range(val2)])
+        d_next = lax.dynamic_update_slice_in_dim(d_next, all_rows, block_now, axis=0)
+    return rings_replace(d_next, local_array)
+
+
+targets_set = functools.partial(search_the_views, which_axis="lat", block_here=1, local_array=0)
 
 
 def dft_table(points, modes, lon_count):
@@ -42,13 +74,7 @@
     dft_basis = dft_table(points, orders.reshape(-1), lon_count).reshape(lon_count, 4 * slot_count)
     fourier = jnp.einsum("ack,kn->anc", masked, dft_basis, preferred_element_type=jnp.float32)
     fourier = (fourier * norm_scale).astype(jnp.bfloat16).reshape(lat_rows, slot_count, 4, chan_dev)
-    received = lax.all_to_all(
-        fourier.reshape(lat_rows, slot_count, 4 * chan_dev),
-        "lat",
-        split_axis=1,
-        concat_axis=0,
-        tiled=True,
-    )
+    received = targets_set(fourier.reshape(lat_rows, slot_count, 4 * chan_dev))
     group_start = lax.axis_index("lat") * group_size
     bound_group = lax.dynamic_slice_in_dim(bound_all, group_start, group_size)
     keep_group = lax.dynamic_slice_in_dim(keep_all, group_start, group_size)

time: 955 us -> 968 us (1.014)
  the two profiles are of different devices: /device:TPU:0 before, /device:TPU:28 now
where the time goes in v1:
time: 968 us; the launch traced here: 963 us
  waiting for transfers between devices  341 us (35%)
  local copies, waits for them, and re-layouts  255 us (26%)
  blocking collectives  209 us (22%)
  matrix products  85.8 us (9%)
  other arithmetic  51.9 us (5%)
  between operations  13.6 us (1%)
    ppermute x7, waiting for transfers between devices, search_the_views(): lax.ppermute(y, which_axis, [(j, (j + dev) % val2) for j in range(val2)])  340 us
    all_to_all x1, blocking collectives, per_device(): lax.all_to_all(part_sums, 'ch', split_axis=0, concat_axis=3, tiled=True)  209 us
    dot_general x1, matrix products, per_device(): jnp.einsum('ack,kn->anc', masked, dft_basis, preferred_element_type=jnp.f...  49.8 us
    another operation x8, local copies, waits for them, and re-layouts  46.4 us
    dynamic_update_slice x8, local copies, waits for them, and re-layouts, search_the_views(): lax.dynamic_update_slice_in_dim(d_next, all_rows, block_now, axis=0)  45.7 us
    dot_general x1, local copies, waits for them, and re-layouts, project(): jnp.einsum('brl,lbn->brn', basis_piece, data_rows, preferred_element_type...  36 us
    dot_general x1, matrix products, project(): jnp.einsum('brl,lbn->brn', basis_piece, data_rows, preferred_element_type...  36 us
    all_to_all x2, local copies, waits for them, and re-layouts, per_device(): lax.all_to_all(part_sums, 'ch', split_axis=0, concat_axis=3, tiled=True)  34.7 us
  transfers between devices with their start and end apart: 8, of which 5 were waited for; matrix products, arithmetic and copies ran while one was open for 28% of the time, Pallas kernels for 0%

profile of v1, /device:TPU:28, one launch (start us, length us, event | category | flops | bytes accessed | tf_op | source)
XLA Modules:
  0.0 963.4 jit_solution(9368798342510541537)
XLA Ops:
  7.7 19.0 %cosine_convert_fusion = (bf16[1440,768,1]{1,0,2:T(8,128)(2,1)S(1)}, bf16[1440,768,1]{1,0,2:T(8,128)(2,1)S(1)}) fusion(s32[768]{0:T(1024)S(1)} %mul.66), kind=kLoop, calls=%fused_computation.18 | loop fusion | flops 13271040 | bytes 4426752 | tf_op jit(solution)/shard_map/convert
  29.9 13.2 %copy.59 = bf16[1440,768,2]{0,2,1:T(2,128)(2,1)} copy(bf16[1440,768,2]{1,0,2:T(8,128)(2,1)} %pad_maximum_fusion) | data formatting | bytes 8847360 | tf_op jit(solution)/shard_map/stack | solution.py:45
  43.1 10.9 %convert_element_type.30 = bf16[1440,1536]{0,1:T(8,128)(2,1)} reshape(bf16[1440,768,2]{0,2,1:T(2,128)(2,1)} %copy.59) | data formatting | bytes 8847360 | tf_op jit(solution)/shard_map/convert_element_type | solution.py:45
  54.0 16.7 %broadcast_select_fusion = bf16[91,64,1440]{2,1,0:T(8,128)(2,1)} fusion(bf16[91,64,1440]{2,1,0:T(8,128)(2,1)} %param.3, pred[91]{0:T(512)(128)(4,1)S(1)} %add_compare_fusion), kind=kLoop, calls=%fused_computation.10 | loop fusion | flops 8386560 | bytes 33546332 | tf_op jit(solution)/shard_map/jit(_where)/select_n | solution.py:71
  70.8 49.8 %fusion = bf16[91,1536,64]{1,0,2:T(8,128)(2,1)} fusion(bf16[91,64,1440]{2,1,0:T(8,128)(2,1)} %broadcast_select_fusion, bf16[1440,1536]{0,1:T(8,128)(2,1)S(1)} %copy-done.5), kind=kOutput, calls=%fused_computation.1 | convolution fusion | flops 25781403648 | bytes 39088128 | tf_op jit(solution)/shard_map/ack,kn->anc/dot_general | solution.py:75
  120.6 31.4 %copy.62 = bf16[91,1536,64]{0,2,1:T(8,128)(2,1)} copy(bf16[91,1536,64]{1,0,2:T(8,128)(2,1)} %fusion) | data formatting | bytes 35782656 | tf_op jit(solution)/shard_map/convert_element_type | solution.py:76
  151.9 14.5 %constant_dynamic-slice_fusion = (bf16[91,1,48,256]{0,3,2,1:T(8,128)(2,1)S(1)}, bf16[91,1,48,256]{0,3,2,1:T(8,128)(2,1)}, bf16[91,1,48,256]{0,3,2,1:T(8,128)(2,1...) fusion(bf16[91,8,48,256]{0,3,2,1:T(8,128)(2,1)} %bitcast.38, ...), kind=kLoop, calls=%fused_computation.25 | loop fusion | bytes 31309852 | tf_op jit(solution)/shard_map/dynamic-slice.6
  166.4 4.9 copy.63
  171.3 4.8 copy.65
  177.9 4.9 copy.67
  184.4 4.8 copy.69
  190.4 4.7 copy.71
  196.9 4.7 copy.73
  204.7 17.3 %collective-permute-done = bf16[1,91,48,256]{3,2,1,0:T(8,128)(2,1)} collective-permute-done((bf16[1,91,48,256]{3,2,1,0:T(8,128)(2,1)}, bf16[1,91,48,256]{3,2,1,0:T(8,128)(2,1)}, u32[]{:S(2)}, u32[]{:S(2)}) %collective-permute-start) | collective-permute-done | bytes 2236448 | tf_op jit(solution)/shard_map/ppermute | solution.py:34
  222.6 47.6 %collective-permute-done.1 = bf16[1,91,48,256]{3,2,1,0:T(8,128)(2,1)} collective-permute-done((bf16[1,91,48,256]{3,2,1,0:T(8,128)(2,1)}, bf16[1,91,48,256]{3,2,1,0:T(8,128)(2,1)}, u32[]{:S(2)}, u32[]{:S(2)}) %collective-permute-start.1) | collective-permute-done | bytes 2236448 | tf_op jit(solution)/shard_map/ppermute | solution.py:34
  270.5 4.7 copy.64
  275.2 3.5 copy.66
  278.7 38.0 %collective-permute-done.2 = bf16[1,91,48,256]{3,2,1,0:T(8,128)(2,1)} collective-permute-done((bf16[1,91,48,256]{3,2,1,0:T(8,128)(2,1)}, bf16[1,91,48,256]{3,2,1,0:T(8,128)(2,1)}, u32[]{:S(2)}, u32[]{:S(2)}) %collective-permute-start.2) | collective-permute-done | bytes 2236448 | tf_op jit(solution)/shard_map/ppermute | solution.py:34
  316.6 4.7 copy.68
  321.4 236.0 %collective-permute-done.3 = bf16[1,91,48,256]{3,2,1,0:T(8,128)(2,1)} collective-permute-done((bf16[1,91,48,256]{3,2,1,0:T(8,128)(2,1)}, bf16[1,91,48,256]{3,2,1,0:T(8,128)(2,1)}, u32[]{:S(2)}, u32[]{:S(2)}) %collective-permute-start.3) | collective-permute-done | bytes 2236448 | tf_op jit(solution)/shard_map/ppermute | solution.py:34
  557.3 4.7 copy.70
  563.4 4.7 copy.72
  568.1 4.6 copy.74
  572.7 4.7 copy.76
  577.5 3.9 constant_dynamic-update-slice_fusion.6
  598.5 29.8 %copy.77 = bf16[8,91,48,256]{3,2,1,0:T(8,128)(2,1)} copy(bf16[8,91,48,256]{1,3,2,0:T(8,128)(2,1)} %constant_dynamic-update-slice_fusion) | data formatting | bytes 35782656 | tf_op jit(solution)/shard_map/dynamic_update_slice | solution.py:35
  628.4 36.0 %fusion.9 = f32[48,721,256]{2,1,0:T(8,128)} fusion(bf16[48,721,728]{2,1,0:T(8,128)(2,1)} %all-gather.2.cloned.1.call-done, bf16[728,48,256]{2,1,0:T(8,128)(2,1)} %bitcast.43), kind=kOutput, calls=%fused_computation.11 | convolution fusion | flops 12899647488 | bytes 103719168 | tf_op jit(solution)/shard_map/brl,lbn->brn/dot_general | solution.py:49
  664.3 36.0 %copy.79 = f32[48,721,256]{1,2,0:T(8,128)} copy(f32[48,721,256]{2,1,0:T(8,128)} %fusion.9) | data formatting | bytes 70877184 | tf_op jit(solution)/shard_map/brl,lbn->brn/dot_general | solution.py:49
  700.4 12.8 %fusion.2 = f32[48,721,2,64]{1,3,2,0:T(8,128)S(1)} fusion(f32[48,721,2,2,64]{1,4,3,2,0:T(8,128)} %bitcast.40, f32[48]{0:T(128)S(1)} %dynamic-slice_convert_fusion, pred[48,721]{1,0:T(8,128)(4,1)S(1)} %iota_compare_fusion), kind=kLoop, calls=%fused_computation.4 | loop fusion | flops 8859648 | bytes 53192688 | tf_op jit(solution)/shard_map/mul | solution.py:57
  713.2 208.6 %all_to_all.18 = f32[48,721,2,64]{1,3,2,0:T(8,128)S(1)} all-to-all(f32[48,721,2,64]{1,3,2,0:T(8,128)S(1)} %fusion.2), channel_id=1, replica_groups=mesh['lat'=8,'ch'=4] {'ch'}, dimensions={0} | all-to-all | bytes 35438592 | tf_op jit(solution)/shard_map/all_to_all | solution.py:84
  921.9 6.9 copy.81
  928.8 27.7 %copy.82 = f32[12,721,2,256]{3,2,1,0:T(2,128)} copy(f32[12,721,2,256]{1,3,2,0:T(8,128)} %bitcast.42) | data formatting | bytes 35438592 | tf_op jit(solution)/shard_map/all_to_all | solution.py:84
  (46 shorter events, 33.1 us)
Async XLA Ops:
  6.5 0.8 copy-start.6
  6.5 621.8 %all-gather.2.cloned.1.call-start = ((), (), s32[]{:S(2)}) async-start(), calls=%async_computation.1 | async-start | bytes 67092480 | tf_op jit(solution)/shard_map/all_gather | solution.py:82
  54.0 16.7 %copy-start.5 = (bf16[1440,1536]{0,1:T(8,128)(2,1)S(1)}, bf16[1440,1536]{0,1:T(8,128)(2,1)}, u32[]{:S(2)}) copy-start(bf16[1440,1536]{0,1:T(8,128)(2,1)} %convert_element_type.30) | copy-start | bytes 13271044
  171.3 50.7 %collective-permute-start = (bf16[1,91,48,256]{3,2,1,0:T(8,128)(2,1)}, bf16[1,91,48,256]{3,2,1,0:T(8,128)(2,1)}, u32[]{:S(2)}, u32[]{:S(2)}) collective-permute-start(bf16[1,91,48,256]{3,2,1,0:T(8,128)(2,1)} %bitcast.50), channel_id=1, source_target_pairs={{0,4},{4,8},{8,12},{12,16},{16,20},{20,24},{24,28},{28,0},{1,5},{5... | collective-permute-start | bytes 6709256 | tf_op jit(solution)/shard_map/ppermute | solution.py:34
  176.2 94.1 %collective-permute-start.1 = (bf16[1,91,48,256]{3,2,1,0:T(8,128)(2,1)}, bf16[1,91,48,256]{3,2,1,0:T(8,128)(2,1)}, u32[]{:S(2)}, u32[]{:S(2)}) collective-permute-start(bf16[1,91,48,256]{3,2,1,0:T(8,128)(2,1)} %bitcast.49), channel_id=1, source_target_pairs={{0,8},{4,12},{8,16},{12,20},{16,24},{20,28},{24,0},{28,4},{1,9},{5... | collective-permute-start | bytes 6709256 | tf_op jit(solution)/shard_map/ppermute | solution.py:34
  182.8 133.9 %collective-permute-start.2 = (bf16[1,91,48,256]{3,2,1,0:T(8,128)(2,1)}, bf16[1,91,48,256]{3,2,1,0:T(8,128)(2,1)}, u32[]{:S(2)}, u32[]{:S(2)}) collective-permute-start(bf16[1,91,48,256]{3,2,1,0:T(8,128)(2,1)} %bitcast.45), channel_id=1, source_target_pairs={{0,12},{4,16},{8,20},{12,24},{16,28},{20,0},{24,4},{28,8},{1,13},{... | collective-permute-start | bytes 6709256 | tf_op jit(solution)/shard_map/ppermute | solution.py:34
  189.2 368.1 %collective-permute-start.3 = (bf16[1,91,48,256]{3,2,1,0:T(8,128)(2,1)}, bf16[1,91,48,256]{3,2,1,0:T(8,128)(2,1)}, u32[]{:S(2)}, u32[]{:S(2)}) collective-permute-start(bf16[1,91,48,256]{3,2,1,0:T(8,128)(2,1)} %bitcast.46), channel_id=1, source_target_pairs={{0,16},{4,20},{8,24},{12,28},{16,0},{20,4},{24,8},{28,12},{1,17},{... | collective-permute-start | bytes 6709256 | tf_op jit(solution)/shard_map/ppermute | solution.py:34
  195.1 368.3 %collective-permute-start.4 = (bf16[1,91,48,256]{3,2,1,0:T(8,128)(2,1)}, bf16[1,91,48,256]{3,2,1,0:T(8,128)(2,1)}, u32[]{:S(2)}, u32[]{:S(2)}) collective-permute-start(bf16[1,91,48,256]{3,2,1,0:T(8,128)(2,1)} %bitcast.47), channel_id=1, source_target_pairs={{0,20},{4,24},{8,28},{12,0},{16,4},{20,8},{24,12},{28,16},{1,21},{... | collective-permute-start | bytes 6709256 | tf_op jit(solution)/shard_map/ppermute | solution.py:34
  222.0 346.1 %collective-permute-start.5 = (bf16[1,91,48,256]{3,2,1,0:T(8,128)(2,1)}, bf16[1,91,48,256]{3,2,1,0:T(8,128)(2,1)}, u32[]{:S(2)}, u32[]{:S(2)}) collective-permute-start(bf16[1,91,48,256]{3,2,1,0:T(8,128)(2,1)} %bitcast.48), channel_id=1, source_target_pairs={{0,24},{4,28},{8,0},{12,4},{16,8},{20,12},{24,16},{28,20},{1,25},{... | collective-permute-start | bytes 6709256 | tf_op jit(solution)/shard_map/ppermute | solution.py:34
  270.2 302.5 %collective-permute-start.6 = (bf16[1,91,48,256]{3,2,1,0:T(8,128)(2,1)}, bf16[1,91,48,256]{3,2,1,0:T(8,128)(2,1)}, u32[]{:S(2)}, u32[]{:S(2)}) collective-permute-start(bf16[1,91,48,256]{3,2,1,0:T(8,128)(2,1)} %bitcast.44), channel_id=1, source_target_pairs={{0,28},{4,0},{8,4},{12,8},{16,12},{20,16},{24,20},{28,24},{1,29},{... | collective-permute-start | bytes 6709256 | tf_op jit(solution)/shard_map/ppermute | solution.py:34
  581.4 3.0 copy-start
  584.4 3.0 copy-start.1
  587.4 3.0 copy-start.2
  590.5 3.0 copy-start.3
  593.5 3.0 copy-start.4
Sparse Core Ops, SparseCore 0:
  8.9 319.0 all-gather.1
